TPU v7x, 128 devices: a whole 4x4x4 slice. The times are simulated.
128 devices in a mesh: wide: 16 (over x_lo, z, core), narrow: 8 (over x_hi, y).
Axes of the slice: x: 4 (x_hi: 2, x_lo: 2; x = x_hi * 2 + x_lo), y: 4, z: 4, core: 2. Of those that a mesh axis runs over, the one named last changes fastest.
Arguments:
- pixel_stack: float32 [128, 128, 4096], P(('wide', 'narrow')), may hold values from -6 to 6
- quality_weight: float32 [128, 128, 4096], P(('wide', 'narrow')), may hold values from 0.2 to 1
Outputs:
- slope: float32 [128, 4096], P('wide', 'narrow')
- level: float32 [128, 4096], P('wide', 'narrow')
- anomaly: bfloat16 [128, 128, 4096], P(None, 'wide', 'narrow')
All inputs are finite; a program needn't handle non-finite values.
Results may differ from a plain program's by a relative error of at most 0.001.
Values sent between devices are 32-bit elements; how exact they have to be, the bound alone decides.
A program may use at most 64 MiB of HBM per device.

v0:
```python
import jax
import jax.numpy as jnp
from jax import lax
from jax.sharding import PartitionSpec as P


def fit_trend(series, weight_series, axis):
    count = series.shape[axis]
    shape = [1] * series.ndim
    shape[axis] = count
    centred = ((jnp.arange(count).astype(jnp.float32) - (count - 1) / 2.0) / count).reshape(shape)
    weighted = weight_series * series
    first = jnp.sum(weight_series, axis=axis, keepdims=True)
    second = jnp.sum(weight_series * centred, axis=axis, keepdims=True)
    third = jnp.sum(weight_series * centred * centred, axis=axis, keepdims=True)
    plain_sum = jnp.sum(weighted, axis=axis, keepdims=True)
    moment_sum = jnp.sum(weighted * centred, axis=axis, keepdims=True)
    determinant = first * third - second * second
    slope = (first * moment_sum - second * plain_sum) / determinant
    level = (third * plain_sum - second * moment_sum) / determinant
    anomaly = (series - level - slope * centred).astype(jnp.bfloat16)
    return (slope, level, anomaly)


def body(pixel_stack, quality_weight):
    wide_count = lax.axis_size("wide")
    narrow_count = lax.axis_size("narrow")
    local_steps = pixel_stack.shape[0]
    rows_tile = pixel_stack.shape[1] // wide_count
    cols_tile = pixel_stack.shape[2] // narrow_count

    def tile_major(field):
        split = field.reshape(local_steps, wide_count, rows_tile, narrow_count, cols_tile)
        return split.transpose(1, 3, 0, 2, 4).reshape(
            wide_count * narrow_count, local_steps, rows_tile, cols_tile
        )

    slope, level, anomaly = fit_trend(
        lax.all_to_all(
            tile_major(pixel_stack), ("wide", "narrow"), split_axis=0, concat_axis=1, tiled=True
        ),
        lax.all_to_all(
            tile_major(quality_weight), ("wide", "narrow"), split_axis=0, concat_axis=1, tiled=True
        ),
        1,
    )
    return (
        slope.reshape(rows_tile, cols_tile),
        level.reshape(rows_tile, cols_tile),
        anomaly.reshape(-1, rows_tile, cols_tile),
    )


def solution(mesh):
    return jax.shard_map(
        body,
        mesh=mesh,
        in_specs=(P(("wide", "narrow"), None, None), P(("wide", "narrow"), None, None)),
        out_specs=(P("wide", "narrow"), P("wide", "narrow"), P(None, "wide", "narrow")),
        check_vma=False,
    )
```

profile of v0, /device:TPU:0, one launch (start us, length us, event | category | flops | bytes accessed | tf_op | source)
XLA Modules:
  0.0 78.9 jit_solution(5695651447361692892)
XLA Ops:
  0.6 40.0 %all_to_all.27 = f32[128,1,8,512]{3,2,1,0:T(8,128)} all-to-all(f32[128,1,8,512]{3,2,1,0:T(8,128)} %bitcast.33), channel_id=1, replica_groups=mesh['wide'=16,'narrow'=8] {'wide','narrow'}, dimensions={0} | all-to-all | bytes 4194304 | tf_op jit(solution)/shard_map/all_to_all | solution.py:42
  40.6 6.1 %all-to-all-start.1 = ((f32[128,1,8,512]{3,2,1,0:T(8,128)}), f32[128,1,8,512]{3,2,1,0:T(8,128)S(1)}, u32[]{:S(2)}, u32[]{:S(2)}) async-start(f32[128,1,8,512]{3,2,1,0:T(8,128)} %bitcast.34), calls=%async_computation.1 | async-start | bytes 4194304 | tf_op jit(solution)/shard_map/all_to_all | solution.py:39
  46.7 1.8 %reduce_sum.45 = f32[8,512]{1,0:T(8,128)S(1)} reduce(f32[128,1,8,512]{3,2,1,0:T(8,128)} %all_to_all.27, f32[]{:T(128)} %constant.2.clone.1), dimensions={0,1}, to_apply=%region_0.0 | reduce | flops 520192 | bytes 2113540 | tf_op jit(solution)/shard_map/reduce_sum | solution.py:13
  48.5 26.9 %all-to-all-done.1 = f32[128,1,8,512]{3,2,1,0:T(8,128)S(1)} async-done(((f32[128,1,8,512]{3,2,1,0:T(8,128)}), f32[128,1,8,512]{3,2,1,0:T(8,128)S(1)}, u32[]{:S(2)}, u32[]{:S(2)}) %all-to-all-start.1) | async-done | bytes 2097184 | tf_op jit(solution)/shard_map/all_to_all | solution.py:39
  75.4 2.2 %multiply_reduce_fusion = (f32[8,512]{1,0:T(8,128)S(1)}, f32[8,512]{1,0:T(8,128)S(1)}, f32[8,512]{1,0:T(8,128)S(1)}, f32[8,512]{1,0:T(8,128)S(1)}) fusion(f32[128,1,8,512]{3,2,1,0:T(8,128)} %all_to_all.27, f32[128]{0:T(128)S(1)} %add_multiply_fusion, f32[128,1,8,512]{3,2,1,0:T(8,128)S(1)} %all-to-all-done.1), kind=kLoop, calls=%fused_computation.5 | loop fusion | flops 4177920 | bytes 4260352 | tf_op jit(solution)/shard_map/reduce_sum | solution.py:15
  77.6 0.0 copy-start
  77.6 0.0 copy-start.1
  77.6 1.3 %fusion.1 = bf16[128,8,512]{2,1,0:T(8,128)(2,1)} fusion(f32[128,1,8,512]{3,2,1,0:T(8,128)S(1)} %all-to-all-done.1, f32[128]{0:T(128)S(1)} %add_multiply_fusion, f32[8,512]{1,0:T(8,128)S(1)} %get-tuple-element.10, f32[8,512]{1,0:T(8,128)S(1)} %get-tuple-element.9), kind=kLoop, calls=%fused_computation.2 | loop fusion | flops 2097152 | bytes 3179008 | tf_op jit(solution)/shard_map/convert_element_type | solution.py:21
  78.9 0.0 copy-done
  78.9 0.0 copy-done.1
  (2 shorter events, 0.0 us)
Async XLA Ops:
  40.6 34.8 %all-to-all-start.1 = ((f32[128,1,8,512]{3,2,1,0:T(8,128)}), f32[128,1,8,512]{3,2,1,0:T(8,128)S(1)}, u32[]{:S(2)}, u32[]{:S(2)}) async-start(f32[128,1,8,512]{3,2,1,0:T(8,128)} %bitcast.34), calls=%async_computation.1 | async-start | bytes 4194304 | tf_op jit(solution)/shard_map/all_to_all | solution.py:39
  77.6 1.3 %copy-start = (f32[8,512]{1,0:T(8,128)}, f32[8,512]{1,0:T(8,128)S(1)}, u32[]{:S(2)}) copy-start(f32[8,512]{1,0:T(8,128)S(1)} %get-tuple-element.9) | copy-start | bytes 49156
  77.6 1.3 %copy-start.1 = (f32[8,512]{1,0:T(8,128)}, f32[8,512]{1,0:T(8,128)S(1)}, u32[]{:S(2)}) copy-start(f32[8,512]{1,0:T(8,128)S(1)} %get-tuple-element.10) | copy-start | bytes 49156
where the time goes:
time: 79.4 us; the launch traced here: 78.9 us
  blocking collectives  40 us (50%)
  waiting for transfers between devices  26.9 us (34%)
  starting transfers between devices  6.08 us (8%)
  other arithmetic  5.26 us (7%)
    all_to_all x1, blocking collectives, body(): lax.all_to_all(tile_major(quality_weight), ('wide', 'narrow'), split_axis...  40 us
    all_to_all x1, waiting for transfers between devices, body(): lax.all_to_all(tile_major(pixel_stack), ('wide', 'narrow'), split_axis=0,...  26.9 us
    all_to_all x1, starting transfers between devices, body(): lax.all_to_all(tile_major(pixel_stack), ('wide', 'narrow'), split_axis=0,...  6.08 us
    reduce_sum x1, other arithmetic, fit_trend(): third = jnp.sum(weight_series * centred * centred, axis=axis, keepdims=True)  2.18 us
    reduce_sum x1, other arithmetic, fit_trend(): first = jnp.sum(weight_series, axis=axis, keepdims=True)  1.78 us
  transfers between devices with their start and end apart: 1, of which 1 were waited for; matrix products, arithmetic and copies ran while one was open for 2% of the time, Pallas kernels for 0%

commit v1 on v0

v1 whole, which is shorter than its diff:
```python
import jax
import jax.numpy as jnp
from jax import lax
from jax.experimental import pallas as pl
from jax.experimental.pallas import tpu as pltpu
from jax.sharding import PartitionSpec as P

MESH = pl.DeviceIdType.MESH
PIECES = 4
LANES = 128
ORDERS = (
    ("xzy", "yzx"),
    ("zyx", "xzy"),
    ("yxz", "zyx"),
    ("xzy", "yxz"),
)
OFFSETS = tuple((u, v) for u in (1, 3, 2, 0) for v in (1, 3, 2, 0) if (u, v) != (0, 0))
OFFSETS = OFFSETS[::4] + OFFSETS[1::4] + OFFSETS[2::4] + OFFSETS[3::4]
VIEWS = {"x": (4, 4), "y": (2, 4, 2), "z": (2, 2, 4)}


def ring(value, shift):
    return lax.rem(value + shift, 4)


def x_parts(x):
    return lax.rem(x, 2), lax.div(x, 2)


def device_of(at, core):
    low, high = x_parts(at["x"])
    return {"wide": low * 8 + at["z"] * 2 + core, "narrow": high * 4 + at["y"]}


def step_of(at, core):
    device = device_of(at, core)
    return device["wide"] * 8 + device["narrow"]


def tile_in_plane(first, at):
    low, high = x_parts(at["x"])
    if first == "x":
        return at["z"] * 4 + at["y"]
    if first == "y":
        return low * 8 + at["z"] * 2 + high
    return low * 8 + high * 4 + at["y"]


def kernel(
    y_ref, w_ref, slope_ref, level_ref, anomaly_ref,
    y_near, w_near, y_all, sums, sums_in, part, part_in, out, fit,
    y_near_sem, w_near_sem, y_all_sem, sums_sem, part_sem, send_sem, out_sem, ready_sem,
):
    wide, narrow = lax.axis_index("wide"), lax.axis_index("narrow")
    core = lax.rem(wide, 2)
    here = {
        "x": lax.div(narrow, 4) * 2 + lax.div(wide, 8),
        "y": lax.rem(narrow, 4),
        "z": lax.rem(lax.div(wide, 2), 4),
    }

    def select(values):
        zero, one = values
        return zero + core * (one - zero)

    def moved(**places):
        return {**here, **places}

    def by_core(function):
        return select([function(c) for c in range(2)])

    def peer_of(piece, shift_second, shift_third):
        places = []
        for c in range(2):
            _, second, third = ORDERS[piece][c]
            at = moved(**{second: ring(here[second], shift_second), third: ring(here[third], shift_third)})
            places.append(device_of(at, c))
        return {axis: select([place[axis] for place in places]) for axis in places[0]}

    def tile_at(piece, u, v):
        def of(c):
            first, second, third = ORDERS[piece][c]
            return tile_in_plane(first, moved(**{second: u, third: v}))

        return by_core(of)

    def place(piece, level):
        return by_core(lambda c: here[ORDERS[piece][c][level]])

    def step_at(piece, slot, u, v):
        def of(c):
            first, second, third = ORDERS[piece][c]
            return step_of(moved(**{first: slot // 2, second: u, third: v}), slot % 2)

        return by_core(of)

    def centred_of(step):
        return (step.astype(jnp.float32) - 63.5) * (1.0 / 128.0)

    barrier = pltpu.get_barrier_semaphore()
    count = 0
    for axis in "xyz":
        for shift in (1, 2, 3):
            for flip in range(2):
                target = device_of(moved(**{axis: ring(here[axis], shift)}), lax.rem(core + flip, 2))
                pl.semaphore_signal(barrier, inc=1, device_id=target, device_id_type=MESH)
                count += 1
    pl.semaphore_signal(barrier, inc=1, device_id=device_of(here, 1 - core), device_id_type=MESH)
    pl.semaphore_wait(barrier, count + 1)

    queues = {"x": [], "y": [], "z": []}
    for piece in range(PIECES):
        for c in range(2):
            first = ORDERS[piece][c][0]
            queues[first] += [(piece, c, shift) for shift in (1, 3, 2, 0)]

    def send_near(piece, c, shift):
        first = ORDERS[piece][c][0]
        where = ring(here[first], shift)
        low, high = x_parts(where)
        slot = here[first] * 2 + core
        for field, near, sem in ((y_ref, y_near, y_near_sem), (w_ref, w_near, w_near_sem)):
            if first == "x":
                source = field.at[low, :, c, high, :, piece]
            elif first == "y":
                source = field.at[:, :, c, :, where, piece]
            else:
                source = field.at[:, where, c, :, :, piece]
            target = near.at[piece, slot].reshape(*VIEWS[first], 8, LANES)

            def remote():
                pltpu.make_async_remote_copy(
                    src_ref=source,
                    dst_ref=target,
                    send_sem=send_sem.at[0],
                    recv_sem=sem.at[piece],
                    device_id=device_of(moved(**{first: where}), c),
                    device_id_type=MESH,
                ).start()

            if shift:
                remote()
            else:

                @pl.when(core == c)
                def _():
                    pltpu.make_async_copy(source, target, sem.at[piece]).start()

                pl.when(core != c)(remote)

    for turn in range(max(len(queue) for queue in queues.values())):
        for axis in "xyz":
            if turn < len(queues[axis]):
                send_near(*queues[axis][turn])

    for axis in "xyz":
        for shift in (1, 2, 3):
            target = device_of(moved(**{axis: ring(here[axis], shift)}), core)
            pl.semaphore_signal(ready_sem, inc=1, device_id=target, device_id_type=MESH)
    pl.semaphore_wait(ready_sem, 9)

    def await_bytes(ref, sem):
        pltpu.make_async_copy(ref, ref, sem).wait()

    def partial_sums(piece):
        own_u, own_v = place(piece, 1), place(piece, 2)
        centred = [centred_of(step_at(piece, slot, own_u, own_v)) for slot in range(8)]

        def one(index, carry):
            u, v = lax.div(index, 4), lax.rem(index, 4)
            tile = tile_at(piece, u, v)
            zero = jnp.zeros((8, LANES), jnp.float32)
            s0, s1, s2, sy, sty = zero, zero, zero, zero, zero
            for slot in range(8):
                w = w_near[piece, slot, tile]
                weighted = w * y_near[piece, slot, tile]
                moment = w * centred[slot]
                s0 += w
                s1 += moment
                s2 += moment * centred[slot]
                sy += weighted
                sty += weighted * centred[slot]
            for i, value in enumerate((s0, s1, s2, sy, sty)):
                sums[piece, u, v, i] = value
            return carry

        lax.fori_loop(0, 16, one, 0)
        own_tile = tile_at(piece, own_u, own_v)
        own_place = own_u * 4 + own_v
        for slot in range(8):
            y_all[piece, own_place, slot] = y_near[piece, slot, own_tile]

    def send_sums(piece):
        own = place(piece, 1)
        for shift in (1, 3, 2):
            pltpu.make_async_remote_copy(
                src_ref=sums.at[piece, ring(own, shift)],
                dst_ref=sums_in.at[piece, shift - 1],
                send_sem=send_sem.at[1],
                recv_sem=sums_sem.at[piece],
                device_id=peer_of(piece, shift, 0),
                device_id_type=MESH,
            ).start()

    def send_series(piece):
        own_u, own_v = place(piece, 1), place(piece, 2)
        own_place = own_u * 4 + own_v
        for du, dv in OFFSETS:
            pltpu.make_async_remote_copy(
                src_ref=y_near.at[piece, :, tile_at(piece, ring(own_u, du), ring(own_v, dv))],
                dst_ref=y_all.at[piece, own_place],
                send_sem=send_sem.at[2],
                recv_sem=y_all_sem.at[piece],
                device_id=peer_of(piece, du, dv),
                device_id_type=MESH,
            ).start()

    def reduce_and_send(piece):
        await_bytes(sums_in.at[piece], sums_sem.at[piece])
        own_u, own_v = place(piece, 1), place(piece, 2)

        def one(v, carry):
            for i in range(5):
                part[piece, v, i] = (sums[piece, own_u, v, i] + sums_in[piece, 0, v, i]) + (
                    sums_in[piece, 1, v, i] + sums_in[piece, 2, v, i]
                )
            return carry

        lax.fori_loop(0, 4, one, 0)
        for shift in (1, 3, 2):
            pltpu.make_async_remote_copy(
                src_ref=part.at[piece, ring(own_v, shift)],
                dst_ref=part_in.at[piece, shift - 1],
                send_sem=send_sem.at[3],
                recv_sem=part_sem.at[piece],
                device_id=peer_of(piece, 0, shift),
                device_id_type=MESH,
            ).start()

    for piece in range(PIECES):
        await_bytes(y_near.at[piece], y_near_sem.at[piece])
        await_bytes(w_near.at[piece], w_near_sem.at[piece])
        partial_sums(piece)
        send_sums(piece)
        send_series(piece)
        if piece:
            reduce_and_send(piece - 1)
    reduce_and_send(PIECES - 1)

    def finish(piece):
        await_bytes(part_in.at[piece], part_sem.at[piece])
        own_v = place(piece, 2)
        s0, s1, s2, sy, sty = (
            (part[piece, own_v, i] + part_in[piece, 0, i]) + (part_in[piece, 1, i] + part_in[piece, 2, i])
            for i in range(5)
        )
        determinant = s0 * s2 - s1 * s1
        slope = (s0 * sty - s1 * sy) / determinant
        level = (s2 * sy - s1 * sty) / determinant
        columns = pl.ds(piece * LANES, LANES)
        fit[0, :, columns] = slope
        fit[1, :, columns] = level
        await_bytes(y_all.at[piece, pl.ds(0, 15)], y_all_sem.at[piece])

        def one(index, carry):
            u, v = lax.div(index, 4), lax.rem(index, 4)
            for slot in range(8):
                step = step_at(piece, slot, u, v)
                rest = y_all[piece, index, slot] - level - slope * centred_of(step)
                out[step, :, columns] = rest.astype(jnp.bfloat16)
            return carry

        lax.fori_loop(0, 16, one, 0)
        pltpu.make_async_copy(out.at[:, :, columns], anomaly_ref.at[:, :, columns], out_sem.at[piece]).start()

    for piece in range(PIECES):
        finish(piece)
    copies = [
        pltpu.make_async_copy(fit.at[0], slope_ref, out_sem.at[PIECES]),
        pltpu.make_async_copy(fit.at[1], level_ref, out_sem.at[PIECES + 1]),
    ]
    for copy in copies:
        copy.start()
    await_bytes(y_near.at[:, pl.ds(0, 7)], send_sem.at[0])
    await_bytes(w_near.at[:, pl.ds(0, 7)], send_sem.at[0])
    await_bytes(sums_in, send_sem.at[1])
    await_bytes(y_all.at[:, pl.ds(0, 15)], send_sem.at[2])
    await_bytes(part_in, send_sem.at[3])
    for piece in range(PIECES):
        columns = pl.ds(piece * LANES, LANES)
        pltpu.make_async_copy(out.at[:, :, columns], anomaly_ref.at[:, :, columns], out_sem.at[piece]).wait()
    for copy in copies:
        copy.wait()


def body(pixel_stack, quality_weight):
    def tiles(field):
        split = field.reshape(2, 4, 2, 8, 2, 4, PIECES, LANES)
        return split.transpose(0, 1, 2, 4, 5, 6, 3, 7)

    f32 = jnp.float32
    tile = (8, LANES)
    return pl.pallas_call(
        kernel,
        out_shape=(
            jax.ShapeDtypeStruct((8, 512), f32),
            jax.ShapeDtypeStruct((8, 512), f32),
            jax.ShapeDtypeStruct((128, 8, 512), jnp.bfloat16),
        ),
        in_specs=[pl.BlockSpec(memory_space=pl.ANY)] * 2,
        out_specs=(pl.BlockSpec(memory_space=pl.ANY),) * 3,
        scratch_shapes=[
            pltpu.VMEM((PIECES, 8, 16, *tile), f32),
            pltpu.VMEM((PIECES, 8, 16, *tile), f32),
            pltpu.VMEM((PIECES, 16, 8, *tile), f32),
            pltpu.VMEM((PIECES, 4, 4, 5, *tile), f32),
            pltpu.VMEM((PIECES, 3, 4, 5, *tile), f32),
            pltpu.VMEM((PIECES, 4, 5, *tile), f32),
            pltpu.VMEM((PIECES, 3, 5, *tile), f32),
            pltpu.VMEM((128, 8, 512), jnp.bfloat16),
            pltpu.VMEM((2, 8, 512), f32),
            pltpu.SemaphoreType.DMA((PIECES,)),
            pltpu.SemaphoreType.DMA((PIECES,)),
            pltpu.SemaphoreType.DMA((PIECES,)),
            pltpu.SemaphoreType.DMA((PIECES,)),
            pltpu.SemaphoreType.DMA((PIECES,)),
            pltpu.SemaphoreType.DMA((4,)),
            pltpu.SemaphoreType.DMA((PIECES + 2,)),
            pltpu.SemaphoreType.REGULAR,
        ],
        compiler_params=pltpu.CompilerParams(collective_id=0, has_side_effects=True),
    )(tiles(pixel_stack), tiles(quality_weight))


def solution(mesh):
    return jax.shard_map(
        body,
        mesh=mesh,
        in_specs=(P(("wide", "narrow"), None, None), P(("wide", "narrow"), None, None)),
        out_specs=(P("wide", "narrow"), P("wide", "narrow"), P(None, "wide", "narrow")),
        check_vma=False,
    )
```

time: 79.4 us -> 60.3 us (0.76)
  Pallas kernels: 0 us -> 54.4 us
  blocking collectives: 40 us -> 0 us
  waiting for transfers between devices: 26.9 us -> 0 us
  starting transfers between devices: 6.08 us -> 0 us
  other arithmetic: 5.26 us -> 0 us
  local copies, waits for them, and re-layouts: 0.01 us -> 4.91 us
    pallas_call x0 -> x1, Pallas kernels: none -> 54.4 us  [body(): pl.pallas_call(kernel, out_shape=(jax.ShapeDtypeStruct((8, 512), f32), ja...]
    all_to_all x1 -> x0, blocking collectives: 40 us -> none  [body(): lax.all_to_all(tile_major(quality_weight), ('wide', 'narrow'), split_axis...]
    all_to_all x1 -> x0, waiting for transfers between devices: 26.9 us -> none  [body(): lax.all_to_all(tile_major(pixel_stack), ('wide', 'narrow'), split_axis=0,...]
    all_to_all x1 -> x0, starting transfers between devices: 6.08 us -> none  [body(): lax.all_to_all(tile_major(pixel_stack), ('wide', 'narrow'), split_axis=0,...]
    unnamed x4 -> x3, local copies, waits for them, and re-layouts: 0.01 us -> 4.91 us
    reduce_sum x2 -> x0, other arithmetic: 3.96 us -> none  [the longest x1 2.18 us: fit_trend(): third = jnp.sum(weight_series * centred * centred, axis=axis, keepdims=True)]
    convert_element_type x1 -> x0, other arithmetic: 1.28 us -> none  [fit_trend(): anomaly = (series - level - slope * centred).astype(jnp.bfloat16)]
  transfers between devices with their start and end apart: 1 -> 0, of which waited for: 1 -> 0; matrix products, arithmetic and copies ran while one was open for 2% -> 0% of each run, Pallas kernels for 0% -> 0%
where the time goes in v1:
time: 60.3 us; the launch traced here: 60 us
  Pallas kernels  54.4 us (90%)
  local copies, waits for them, and re-layouts  4.91 us (8%)
  between operations  0.64 us (1%)
    pallas_call x1, Pallas kernels, body(): pl.pallas_call(kernel, out_shape=(jax.ShapeDtypeStruct((8, 512), f32), ja...  54.4 us
    unnamed x3, local copies, waits for them, and re-layouts  4.91 us

profile of v1, /device:TPU:0, one launch (start us, length us, event | category | flops | bytes accessed | tf_op | source)
XLA Modules:
  0.0 60.0 jit_solution(11967260169990080383)
XLA Ops:
  0.6 54.4 %shard_map.49 = (f32[8,512]{1,0:T(8,128)}, f32[8,512]{1,0:T(8,128)}, bf16[128,8,512]{2,1,0:T(8,128)(2,1)}) custom-call(f32[2,4,2,2,4,4,8,128]{7,6,5,4,3,2,1,0:T(8,128)} %bitcast.6, f32[2,4,2,2,4,4,8,128]{7,6,5,4,3,2,1,0:T(8,128)} %bitcast.7), custom_call_target="tpu_custom_call" | custom-call | tf_op jit(solution)/shard_map/pallas_call | solution.py:303
  55.1 1.3 %copy.8 = f32[8,512]{1,0:T(8,128)} copy(f32[8,512]{1,0:T(8,128)} %get-tuple-element.6) | data formatting | bytes 32768
  56.4 1.3 %copy.9 = f32[8,512]{1,0:T(8,128)} copy(f32[8,512]{1,0:T(8,128)} %get-tuple-element.7) | data formatting | bytes 32768
  57.7 2.3 %copy.10 = bf16[128,8,512]{2,1,0:T(8,128)(2,1)} copy(bf16[128,8,512]{2,1,0:T(8,128)(2,1)} %get-tuple-element.8) | data formatting | bytes 2097152

commit v2 on v1

--- a/solution.py
+++ b/solution.py
@@ -48,8 +48,8 @@
 
 def kernel(
     y_ref, w_ref, slope_ref, level_ref, anomaly_ref,
-    y_near, w_near, y_all, sums, sums_in, part, part_in, out, fit,
-    y_near_sem, w_near_sem, y_all_sem, sums_sem, part_sem, send_sem, out_sem, ready_sem,
+    y_near, w_near, y_all, sums, sums_in, part, part_in,
+    y_near_sem, w_near_sem, y_all_sem, sums_sem, part_sem, send_sem, ready_sem,
 ):
     wide, narrow = lax.axis_index("wide"), lax.axis_index("narrow")
     core = lax.rem(wide, 2)
@@ -243,9 +243,8 @@
         partial_sums(piece)
         send_sums(piece)
         send_series(piece)
-        if piece:
-            reduce_and_send(piece - 1)
-    reduce_and_send(PIECES - 1)
+    for piece in range(PIECES):
+        reduce_and_send(piece)
 
     def finish(piece):
         await_bytes(part_in.at[piece], part_sem.at[piece])
@@ -258,8 +257,8 @@
         slope = (s0 * sty - s1 * sy) / determinant
         level = (s2 * sy - s1 * sty) / determinant
         columns = pl.ds(piece * LANES, LANES)
-        fit[0, :, columns] = slope
-        fit[1, :, columns] = level
+        slope_ref[:, columns] = slope
+        level_ref[:, columns] = level
         await_bytes(y_all.at[piece, pl.ds(0, 15)], y_all_sem.at[piece])
 
         def one(index, carry):
@@ -267,30 +266,18 @@
             for slot in range(8):
                 step = step_at(piece, slot, u, v)
                 rest = y_all[piece, index, slot] - level - slope * centred_of(step)
-                out[step, :, columns] = rest.astype(jnp.bfloat16)
+                anomaly_ref[step, :, columns] = rest.astype(jnp.bfloat16)
             return carry
 
         lax.fori_loop(0, 16, one, 0)
-        pltpu.make_async_copy(out.at[:, :, columns], anomaly_ref.at[:, :, columns], out_sem.at[piece]).start()
 
     for piece in range(PIECES):
         finish(piece)
-    copies = [
-        pltpu.make_async_copy(fit.at[0], slope_ref, out_sem.at[PIECES]),
-        pltpu.make_async_copy(fit.at[1], level_ref, out_sem.at[PIECES + 1]),
-    ]
-    for copy in copies:
-        copy.start()
     await_bytes(y_near.at[:, pl.ds(0, 7)], send_sem.at[0])
     await_bytes(w_near.at[:, pl.ds(0, 7)], send_sem.at[0])
     await_bytes(sums_in, send_sem.at[1])
     await_bytes(y_all.at[:, pl.ds(0, 15)], send_sem.at[2])
     await_bytes(part_in, send_sem.at[3])
-    for piece in range(PIECES):
-        columns = pl.ds(piece * LANES, LANES)
-        pltpu.make_async_copy(out.at[:, :, columns], anomaly_ref.at[:, :, columns], out_sem.at[piece]).wait()
-    for copy in copies:
-        copy.wait()
 
 
 def body(pixel_stack, quality_weight):
@@ -303,12 +290,12 @@
     return pl.pallas_call(
         kernel,
         out_shape=(
-            jax.ShapeDtypeStruct((8, 512), f32),
-            jax.ShapeDtypeStruct((8, 512), f32),
-            jax.ShapeDtypeStruct((128, 8, 512), jnp.bfloat16),
+            pltpu.VMEM((8, 512), f32),
+            pltpu.VMEM((8, 512), f32),
+            pltpu.VMEM((128, 8, 512), jnp.bfloat16),
         ),
         in_specs=[pl.BlockSpec(memory_space=pl.ANY)] * 2,
-        out_specs=(pl.BlockSpec(memory_space=pl.ANY),) * 3,
+        out_specs=(pl.BlockSpec(memory_space=pltpu.VMEM),) * 3,
         scratch_shapes=[
             pltpu.VMEM((PIECES, 8, 16, *tile), f32),
             pltpu.VMEM((PIECES, 8, 16, *tile), f32),
@@ -317,15 +304,12 @@
             pltpu.VMEM((PIECES, 3, 4, 5, *tile), f32),
             pltpu.VMEM((PIECES, 4, 5, *tile), f32),
             pltpu.VMEM((PIECES, 3, 5, *tile), f32),
-            pltpu.VMEM((128, 8, 512), jnp.bfloat16),
-            pltpu.VMEM((2, 8, 512), f32),
             pltpu.SemaphoreType.DMA((PIECES,)),
             pltpu.SemaphoreType.DMA((PIECES,)),
             pltpu.SemaphoreType.DMA((PIECES,)),
             pltpu.SemaphoreType.DMA((PIECES,)),
             pltpu.SemaphoreType.DMA((PIECES,)),
             pltpu.SemaphoreType.DMA((4,)),
-            pltpu.SemaphoreType.DMA((PIECES + 2,)),
             pltpu.SemaphoreType.REGULAR,
         ],
         compiler_params=pltpu.CompilerParams(collective_id=0, has_side_effects=True),

time: 60.3 us -> 51 us (0.85)
  Pallas kernels: 54.4 us -> 47.8 us
  local copies, waits for them, and re-layouts: 4.91 us -> 2.18 us
    pallas_call x1, Pallas kernels: 54.4 us -> 47.8 us  [body(): pl.pallas_call(kernel, out_shape=(pltpu.VMEM((8, 512), f32), pltpu.VMEM((...]
    unnamed x3, local copies, waits for them, and re-layouts: 4.91 us -> 2.18 us
where the time goes in v2:
time: 51 us; the launch traced here: 50.6 us
  Pallas kernels  47.8 us (94%)
  local copies, waits for them, and re-layouts  2.18 us (4%)
  between operations  0.64 us (1%)
    pallas_call x1, Pallas kernels, body(): pl.pallas_call(kernel, out_shape=(pltpu.VMEM((8, 512), f32), pltpu.VMEM((...  47.8 us
    unnamed x3, local copies, waits for them, and re-layouts  2.18 us

profile of v2, /device:TPU:0, one launch (start us, length us, event | category | flops | bytes accessed | tf_op | source)
XLA Modules:
  0.0 50.6 jit_solution(9766752805231349914)
XLA Ops:
  0.6 47.8 %shard_map.49 = (f32[8,512]{1,0:T(8,128)S(1)}, f32[8,512]{1,0:T(8,128)S(1)}, bf16[128,8,512]{2,1,0:T(8,128)(2,1)S(1)}) custom-call(f32[2,4,2,2,4,4,8,128]{7,6,5,4,3,2,1,0:T(8,128)} %bitcast.6, f32[2,4,2,2,4,4,8,128]{7,6,5,4,3,2,1,0:T(8,128)} %bitcast.7), custom_call_target="tpu_custom_call" | custom-call | tf_op jit(solution)/shard_map/pallas_call | solution.py:290
  48.4 0.6 %copy.8 = f32[8,512]{1,0:T(8,128)} copy(f32[8,512]{1,0:T(8,128)S(1)} %get-tuple-element.3) | data formatting | bytes 32768
  49.0 0.6 %copy.9 = f32[8,512]{1,0:T(8,128)} copy(f32[8,512]{1,0:T(8,128)S(1)} %get-tuple-element.4) | data formatting | bytes 32768
  49.6 1.0 %copy.10 = bf16[128,8,512]{2,1,0:T(8,128)(2,1)} copy(bf16[128,8,512]{2,1,0:T(8,128)(2,1)S(1)} %get-tuple-element.5) | data formatting | bytes 2097152

commit v3 on v2

--- a/solution.py
+++ b/solution.py
@@ -16,6 +16,7 @@
 )
 OFFSETS = tuple((u, v) for u in (1, 3, 2, 0) for v in (1, 3, 2, 0) if (u, v) != (0, 0))
 OFFSETS = OFFSETS[::4] + OFFSETS[1::4] + OFFSETS[2::4] + OFFSETS[3::4]
+SCHEDULE = "G0 G1 Y0 G2 Y1 G3 Y2 Y3 B0 B1 B2 B3 F0 F1 F2 F3"
 VIEWS = {"x": (4, 4), "y": (2, 4, 2), "z": (2, 2, 4)}
 
 
@@ -237,14 +238,11 @@
                 device_id_type=MESH,
             ).start()
 
-    for piece in range(PIECES):
+    def gather(piece):
         await_bytes(y_near.at[piece], y_near_sem.at[piece])
         await_bytes(w_near.at[piece], w_near_sem.at[piece])
         partial_sums(piece)
         send_sums(piece)
-        send_series(piece)
-    for piece in range(PIECES):
-        reduce_and_send(piece)
 
     def finish(piece):
         await_bytes(part_in.at[piece], part_sem.at[piece])
@@ -261,18 +259,23 @@
         level_ref[:, columns] = level
         await_bytes(y_all.at[piece, pl.ds(0, 15)], y_all_sem.at[piece])
 
+        start = step_at(piece, 0, 0, 0)
+        ahead = [step_at(piece, slot, 0, 0) - start for slot in range(8)]
+        trend = [slope * centred_of(start + shift) for shift in ahead]
+
         def one(index, carry):
-            u, v = lax.div(index, 4), lax.rem(index, 4)
+            first_step = step_at(piece, 0, lax.div(index, 4), lax.rem(index, 4))
+            rise = slope * ((first_step - start).astype(jnp.float32) * (1.0 / 128.0))
             for slot in range(8):
-                step = step_at(piece, slot, u, v)
-                rest = y_all[piece, index, slot] - level - slope * centred_of(step)
-                anomaly_ref[step, :, columns] = rest.astype(jnp.bfloat16)
+                rest = (y_all[piece, index, slot] - level) - (trend[slot] + rise)
+                anomaly_ref[first_step + ahead[slot], :, columns] = rest.astype(jnp.bfloat16)
             return carry
 
         lax.fori_loop(0, 16, one, 0)
 
-    for piece in range(PIECES):
-        finish(piece)
+    phases = {"G": gather, "Y": send_series, "B": reduce_and_send, "F": finish}
+    for name in SCHEDULE.split():
+        phases[name[0]](int(name[1]))
     await_bytes(y_near.at[:, pl.ds(0, 7)], send_sem.at[0])
     await_bytes(w_near.at[:, pl.ds(0, 7)], send_sem.at[0])
     await_bytes(sums_in, send_sem.at[1])
@@ -280,6 +283,15 @@
     await_bytes(part_in, send_sem.at[3])
 
 
+def store(slope_ref, level_ref, anomaly_ref, slope_out, level_out, anomaly_out, sem):
+    pairs = ((anomaly_ref, anomaly_out), (slope_ref, slope_out), (level_ref, level_out))
+    copies = [pltpu.make_async_copy(source, target, sem.at[i]) for i, (source, target) in enumerate(pairs)]
+    for copy in copies:
+        copy.start()
+    for copy in copies:
+        copy.wait()
+
+
 def body(pixel_stack, quality_weight):
     def tiles(field):
         split = field.reshape(2, 4, 2, 8, 2, 4, PIECES, LANES)
@@ -287,7 +299,7 @@
 
     f32 = jnp.float32
     tile = (8, LANES)
-    return pl.pallas_call(
+    fitted = pl.pallas_call(
         kernel,
         out_shape=(
             pltpu.VMEM((8, 512), f32),
@@ -314,6 +326,13 @@
         ],
         compiler_params=pltpu.CompilerParams(collective_id=0, has_side_effects=True),
     )(tiles(pixel_stack), tiles(quality_weight))
+    return pl.pallas_call(
+        store,
+        out_shape=tuple(jax.ShapeDtypeStruct(field.shape, field.dtype) for field in fitted),
+        in_specs=[pl.BlockSpec(memory_space=pltpu.VMEM)] * 3,
+        out_specs=(pl.BlockSpec(memory_space=pl.ANY),) * 3,
+        scratch_shapes=[pltpu.SemaphoreType.DMA((3,))],
+    )(*(pltpu.with_memory_space_constraint(field, pltpu.VMEM) for field in fitted))
 
 
 def solution(mesh):

time: 51 us -> 48.6 us (0.953)
  local copies, waits for them, and re-layouts: 2.18 us -> 0 us
    unnamed x3 -> x0, local copies, waits for them, and re-layouts: 2.18 us -> none
    pallas_call x1, Pallas kernels: 47.8 us -> 46.4 us  [body(): pl.pallas_call(kernel, out_shape=(pltpu.VMEM((8, 512), f32), pltpu.VMEM((...]
    pallas_call x0 -> x1, Pallas kernels: none -> 1 us  [body(): pl.pallas_call(store, out_shape=tuple((jax.ShapeDtypeStruct(field.shape,...]
where the time goes in v3:
time: 48.6 us; the launch traced here: 48 us
  Pallas kernels  47.4 us (98%)
  between operations  0.64 us (1%)
    pallas_call x1, Pallas kernels, body(): pl.pallas_call(kernel, out_shape=(pltpu.VMEM((8, 512), f32), pltpu.VMEM((...  46.4 us
    pallas_call x1, Pallas kernels, body(): pl.pallas_call(store, out_shape=tuple((jax.ShapeDtypeStruct(field.shape,...  1 us

profile of v3, /device:TPU:0, one launch (start us, length us, event | category | flops | bytes accessed | tf_op | source)
XLA Modules:
  0.0 48.0 jit_solution(13452849822559481667)
XLA Ops:
  0.6 46.4 %shard_map.49 = (f32[8,512]{1,0:T(8,128)S(1)}, f32[8,512]{1,0:T(8,128)S(1)}, bf16[128,8,512]{2,1,0:T(8,128)(2,1)S(1)}) custom-call(f32[2,4,2,2,4,4,8,128]{7,6,5,4,3,2,1,0:T(8,128)} %bitcast.6, f32[2,4,2,2,4,4,8,128]{7,6,5,4,3,2,1,0:T(8,128)} %bitcast.7), custom_call_target="tpu_custom_call" | custom-call | tf_op jit(solution)/shard_map/pallas_call | solution.py:302
  47.0 1.0 %shard_map.50 = (f32[8,512]{1,0:T(8,128)}, f32[8,512]{1,0:T(8,128)}, bf16[128,8,512]{2,1,0:T(8,128)(2,1)}) custom-call(f32[8,512]{1,0:T(8,128)S(1)} %get-tuple-element.6.slope_ref, f32[8,512]{1,0:T(8,128)S(1)} %get-tuple-element.7.level_ref, bf16[128,8,512]{2,1,0:T(8,128)(2,1)S(1)} %get-tuple-element.8.anomaly_ref), custom_call_target="tpu_custom_call" | custom-call | tf_op jit(solution)/shard_map/pallas_call | solution.py:329

commit v4 on v3

--- a/solution.py
+++ b/solution.py
@@ -1,3 +1,5 @@
+import functools
+
 import jax
 import jax.numpy as jnp
 from jax import lax
@@ -8,15 +10,10 @@
 MESH = pl.DeviceIdType.MESH
 PIECES = 4
 LANES = 128
-ORDERS = (
-    ("xzy", "yzx"),
-    ("zyx", "xzy"),
-    ("yxz", "zyx"),
-    ("xzy", "yxz"),
-)
-OFFSETS = tuple((u, v) for u in (1, 3, 2, 0) for v in (1, 3, 2, 0) if (u, v) != (0, 0))
-OFFSETS = OFFSETS[::4] + OFFSETS[1::4] + OFFSETS[2::4] + OFFSETS[3::4]
-SCHEDULE = "G0 G1 Y0 G2 Y1 G3 Y2 Y3 B0 B1 B2 B3 F0 F1 F2 F3"
+ORDERS = (("xzy", "yzx"), ("zyx", "xzy"), ("yxz", "zyx"), ("xzy", "yxz"))
+OFFSETS = ((0, 0), (0, 1), (1, 0), (0, None), (None, 0), (0, 2), (1, 1), (2, 0), (None, 1), (1, None), (1, 2), (2, 1), (None, 2), (2, None), (2, 2))
+TURNS = ((0, 0), (0, 1), (1, 0), (1, 1), (2, 0), (2, 1), (None, 0), (None, 1))
+SCHEDULE = ("S0S1S2S3", "R", "G0", "G1", "Y0", "G2", "Y1", "G3", "Y2", "P3", "B0", "B1", "B2", "B3", "Q3", "F0", "F1", "F2", "F3")
 VIEWS = {"x": (4, 4), "y": (2, 4, 2), "z": (2, 2, 4)}
 
 
@@ -50,7 +47,7 @@
 def kernel(
     y_ref, w_ref, slope_ref, level_ref, anomaly_ref,
     y_near, w_near, y_all, sums, sums_in, part, part_in,
-    y_near_sem, w_near_sem, y_all_sem, sums_sem, part_sem, send_sem, ready_sem,
+    y_near_sem, w_near_sem, y_all_sem, sums_sem, part_sem, send_sem, seen_sem, ready_sem,
 ):
     wide, narrow = lax.axis_index("wide"), lax.axis_index("narrow")
     core = lax.rem(wide, 2)
@@ -99,66 +96,95 @@
         return (step.astype(jnp.float32) - 63.5) * (1.0 / 128.0)
 
     barrier = pltpu.get_barrier_semaphore()
-    count = 0
-    for axis in "xyz":
-        for shift in (1, 2, 3):
-            for flip in range(2):
-                target = device_of(moved(**{axis: ring(here[axis], shift)}), lax.rem(core + flip, 2))
-                pl.semaphore_signal(barrier, inc=1, device_id=target, device_id_type=MESH)
-                count += 1
-    pl.semaphore_signal(barrier, inc=1, device_id=device_of(here, 1 - core), device_id_type=MESH)
-    pl.semaphore_wait(barrier, count + 1)
-
-    queues = {"x": [], "y": [], "z": []}
-    for piece in range(PIECES):
-        for c in range(2):
-            first = ORDERS[piece][c][0]
-            queues[first] += [(piece, c, shift) for shift in (1, 3, 2, 0)]
-
-    def send_near(piece, c, shift):
+
+    def greet(condition, semaphore, target):
+        @pl.when(condition)
+        def _():
+            pl.semaphore_signal(semaphore, inc=1, device_id=target, device_id_type=MESH)
+
+    everyone = [(n, axis, q, c) for n, axis in enumerate("xyz") for q in range(4) for c in range(2)]
+    for _, axis, q, c in everyone:
+        greet(here[axis] < q, barrier, device_of(moved(**{axis: q}), c))
+    greet(core == 1, barrier, device_of(here, 0))
+    before = 2 * (here["x"] + here["y"] + here["z"]) + (1 - core)
+
+    @pl.when(before > 0)
+    def _():
+        pl.semaphore_wait(barrier, before)
+
+    for n, axis, q, c in everyone:
+        greet(q < here[axis], seen_sem.at[8 * n + 2 * here[axis] + core], device_of(moved(**{axis: q}), c))
+    greet(core == 0, seen_sem.at[24], device_of(here, 1))
+    heard = set()
+
+    def hear(condition, key, index):
+        if key not in heard:
+            heard.add(key)
+
+            @pl.when(condition)
+            def _():
+                pl.semaphore_wait(seen_sem.at[index], 1)
+
+    def mirrored(shift):
+        return shift
+
+    def near_copy(piece, c, shift, which):
         first = ORDERS[piece][c][0]
-        where = ring(here[first], shift)
+        where = here[first] if shift is None else nth(here[first], shift)
         low, high = x_parts(where)
-        slot = here[first] * 2 + core
-        for field, near, sem in ((y_ref, y_near, y_near_sem), (w_ref, w_near, w_near_sem)):
-            if first == "x":
-                source = field.at[low, :, c, high, :, piece]
-            elif first == "y":
-                source = field.at[:, :, c, :, where, piece]
-            else:
-                source = field.at[:, where, c, :, :, piece]
-            target = near.at[piece, slot].reshape(*VIEWS[first], 8, LANES)
-
-            def remote():
-                pltpu.make_async_remote_copy(
-                    src_ref=source,
-                    dst_ref=target,
-                    send_sem=send_sem.at[0],
-                    recv_sem=sem.at[piece],
-                    device_id=device_of(moved(**{first: where}), c),
-                    device_id_type=MESH,
-                ).start()
-
-            if shift:
-                remote()
-            else:
-
-                @pl.when(core == c)
-                def _():
-                    pltpu.make_async_copy(source, target, sem.at[piece]).start()
-
-                pl.when(core != c)(remote)
-
-    for turn in range(max(len(queue) for queue in queues.values())):
+        field, near, sem = ((y_ref, y_near, y_near_sem), (w_ref, w_near, w_near_sem))[which]
+        if first == "x":
+            source = field.at[low, :, c, high, :, piece]
+        elif first == "y":
+            source = field.at[:, :, c, :, where, piece]
+        else:
+            source = field.at[:, where, c, :, :, piece]
+        target = near.at[piece, here[first] * 2 + core].reshape(*VIEWS[first], 8, LANES)
+
+        def remote():
+            pltpu.make_async_remote_copy(
+                src_ref=source,
+                dst_ref=target,
+                send_sem=send_sem.at[0],
+                recv_sem=sem.at[piece],
+                device_id=device_of(moved(**{first: where}), c),
+                device_id_type=MESH,
+            ).start()
+
+        if shift is not None:
+            hear(here[first] <= shift, (first, shift, c), 8 * "xyz".index(first) + 2 * where + c)
+            remote()
+        else:
+
+            @pl.when(core == c)
+            def _():
+                pltpu.make_async_copy(source, target, sem.at[piece]).start()
+
+            if c == 0:
+                hear(core == 1, c, 24)
+            pl.when(core != c)(remote)
+
+    def nth(own, k):
+        return own if k is None else k + (own <= k).astype(jnp.int32)
+
+    def near_copies(pieces):
+        queues = {"x": [], "y": [], "z": []}
+        for piece in pieces:
+            for shift, which in ((0, 0), (0, 1), (1, 0), (1, 1), (2, 0), (2, 1), (None, 0), (None, 1)):
+                for c in range(2):
+                    queues[ORDERS[piece][c][0]].append(functools.partial(near_copy, piece, c, shift, which))
+        return merge([queue for queue in queues.values() if queue])
+
+    def merge(lists):
+        ranked = [((i + 0.5) / len(items), n, item) for n, items in enumerate(lists) for i, item in enumerate(items)]
+        return [item for _, _, item in sorted(ranked, key=lambda entry: entry[:2])]
+
+    def await_partners():
         for axis in "xyz":
-            if turn < len(queues[axis]):
-                send_near(*queues[axis][turn])
-
-    for axis in "xyz":
-        for shift in (1, 2, 3):
-            target = device_of(moved(**{axis: ring(here[axis], shift)}), core)
-            pl.semaphore_signal(ready_sem, inc=1, device_id=target, device_id_type=MESH)
-    pl.semaphore_wait(ready_sem, 9)
+            for shift in (1, 2, 3):
+                target = device_of(moved(**{axis: ring(here[axis], shift)}), core)
+                pl.semaphore_signal(ready_sem, inc=1, device_id=target, device_id_type=MESH)
+        pl.semaphore_wait(ready_sem, 9)
 
     def await_bytes(ref, sem):
         pltpu.make_async_copy(ref, ref, sem).wait()
@@ -193,28 +219,32 @@
 
     def send_sums(piece):
         own = place(piece, 1)
-        for shift in (1, 3, 2):
+        for n in range(3):
+            u = nth(own, n)
             pltpu.make_async_remote_copy(
-                src_ref=sums.at[piece, ring(own, shift)],
-                dst_ref=sums_in.at[piece, shift - 1],
+                src_ref=sums.at[piece, u],
+                dst_ref=sums_in.at[piece, own - (u < own).astype(jnp.int32)],
                 send_sem=send_sem.at[1],
                 recv_sem=sums_sem.at[piece],
-                device_id=peer_of(piece, shift, 0),
+                device_id=peer_of(piece, u - own + 4, 0),
                 device_id_type=MESH,
             ).start()
 
-    def send_series(piece):
+    def series_copy(piece, du, dv):
         own_u, own_v = place(piece, 1), place(piece, 2)
-        own_place = own_u * 4 + own_v
-        for du, dv in OFFSETS:
-            pltpu.make_async_remote_copy(
-                src_ref=y_near.at[piece, :, tile_at(piece, ring(own_u, du), ring(own_v, dv))],
-                dst_ref=y_all.at[piece, own_place],
-                send_sem=send_sem.at[2],
-                recv_sem=y_all_sem.at[piece],
-                device_id=peer_of(piece, du, dv),
-                device_id_type=MESH,
-            ).start()
+        u, v = nth(own_u, du), nth(own_v, dv)
+        pltpu.make_async_remote_copy(
+            src_ref=y_near.at[piece, :, tile_at(piece, u, v)],
+            dst_ref=y_all.at[piece, own_u * 4 + own_v],
+            send_sem=send_sem.at[2],
+            recv_sem=y_all_sem.at[piece],
+            device_id=peer_of(piece, u - own_u + 4, v - own_v + 4),
+            device_id_type=MESH,
+        ).start()
+
+    def series_copies(kind, piece):
+        part = {"Y": OFFSETS, "P": OFFSETS[:11], "Q": OFFSETS[11:]}[kind]
+        return [functools.partial(series_copy, piece, du, dv) for du, dv in part]
 
     def reduce_and_send(piece):
         await_bytes(sums_in.at[piece], sums_sem.at[piece])
@@ -228,13 +258,14 @@
             return carry
 
         lax.fori_loop(0, 4, one, 0)
-        for shift in (1, 3, 2):
+        for n in range(3):
+            v = nth(own_v, n)
             pltpu.make_async_remote_copy(
-                src_ref=part.at[piece, ring(own_v, shift)],
-                dst_ref=part_in.at[piece, shift - 1],
+                src_ref=part.at[piece, v],
+                dst_ref=part_in.at[piece, own_v - (v < own_v).astype(jnp.int32)],
                 send_sem=send_sem.at[3],
                 recv_sem=part_sem.at[piece],
-                device_id=peer_of(piece, 0, shift),
+                device_id=peer_of(piece, 0, v - own_v + 4),
                 device_id_type=MESH,
             ).start()
 
@@ -273,9 +304,19 @@
 
         lax.fori_loop(0, 16, one, 0)
 
-    phases = {"G": gather, "Y": send_series, "B": reduce_and_send, "F": finish}
-    for name in SCHEDULE.split():
-        phases[name[0]](int(name[1]))
+    steps = {"G": gather, "B": reduce_and_send, "F": finish}
+    for name in SCHEDULE:
+        if name == "R":
+            await_partners()
+        elif name[0] in steps:
+            steps[name[0]](int(name[1]))
+        else:
+            pairs = [(name[i], int(name[i + 1])) for i in range(0, len(name), 2)]
+            near = [piece for kind, piece in pairs if kind == "S"]
+            lists = [near_copies(near)] if near else []
+            for copy in merge(lists + [series_copies(kind, piece) for kind, piece in pairs if kind != "S"]):
+                copy()
+
     await_bytes(y_near.at[:, pl.ds(0, 7)], send_sem.at[0])
     await_bytes(w_near.at[:, pl.ds(0, 7)], send_sem.at[0])
     await_bytes(sums_in, send_sem.at[1])
@@ -322,6 +363,7 @@
             pltpu.SemaphoreType.DMA((PIECES,)),
             pltpu.SemaphoreType.DMA((PIECES,)),
             pltpu.SemaphoreType.DMA((4,)),
+            pltpu.SemaphoreType.REGULAR((25,)),
             pltpu.SemaphoreType.REGULAR,
         ],
         compiler_params=pltpu.CompilerParams(collective_id=0, has_side_effects=True),

time: 48.6 us -> 47.9 us (0.986)
  the two profiles are of different devices: /device:TPU:0 before, /device:TPU:56 now
where the time goes in v4:
time: 47.9 us; the launch traced here: 47.8 us
  Pallas kernels  47.1 us (98%)
  between operations  0.64 us (1%)
    pallas_call x1, Pallas kernels, body(): pl.pallas_call(kernel, out_shape=(pltpu.VMEM((8, 512), f32), pltpu.VMEM((...  46.1 us
    pallas_call x1, Pallas kernels, body(): pl.pallas_call(store, out_shape=tuple((jax.ShapeDtypeStruct(field.shape,...  1 us

profile of v4, /device:TPU:56, one launch (start us, length us, event | category | flops | bytes accessed | tf_op | source)
XLA Modules:
  0.0 47.8 jit_solution(4989382165408217035)
XLA Ops:
  0.6 46.1 %shard_map.49 = (f32[8,512]{1,0:T(8,128)S(1)}, f32[8,512]{1,0:T(8,128)S(1)}, bf16[128,8,512]{2,1,0:T(8,128)(2,1)S(1)}) custom-call(f32[2,4,2,2,4,4,8,128]{7,6,5,4,3,2,1,0:T(8,128)} %bitcast.6, f32[2,4,2,2,4,4,8,128]{7,6,5,4,3,2,1,0:T(8,128)} %bitcast.7), custom_call_target="tpu_custom_call" | custom-call | tf_op jit(solution)/shard_map/pallas_call | solution.py:343
  46.8 1.0 %shard_map.50 = (f32[8,512]{1,0:T(8,128)}, f32[8,512]{1,0:T(8,128)}, bf16[128,8,512]{2,1,0:T(8,128)(2,1)}) custom-call(f32[8,512]{1,0:T(8,128)S(1)} %get-tuple-element.6.slope_ref, f32[8,512]{1,0:T(8,128)S(1)} %get-tuple-element.7.level_ref, bf16[128,8,512]{2,1,0:T(8,128)(2,1)S(1)} %get-tuple-element.8.anomaly_ref), custom_call_target="tpu_custom_call" | custom-call | tf_op jit(solution)/shard_map/pallas_call | solution.py:371

commit v5 on v4

--- a/solution.py
+++ b/solution.py
@@ -13,7 +13,7 @@
 ORDERS = (("xzy", "yzx"), ("zyx", "xzy"), ("yxz", "zyx"), ("xzy", "yxz"))
 OFFSETS = ((0, 0), (0, 1), (1, 0), (0, None), (None, 0), (0, 2), (1, 1), (2, 0), (None, 1), (1, None), (1, 2), (2, 1), (None, 2), (2, None), (2, 2))
 TURNS = ((0, 0), (0, 1), (1, 0), (1, 1), (2, 0), (2, 1), (None, 0), (None, 1))
-SCHEDULE = ("S0S1S2S3", "R", "G0", "G1", "Y0", "G2", "Y1", "G3", "Y2", "P3", "B0", "B1", "B2", "B3", "Q3", "F0", "F1", "F2", "F3")
+SCHEDULE = ("S0S1S2", "R", "S3", "G0", "G1", "Y0", "G2", "Y1", "G3", "Y2", "P3", "B0", "B1", "B2", "B3", "Q3", "F0", "F1", "F2", "F3")
 VIEWS = {"x": (4, 4), "y": (2, 4, 2), "z": (2, 2, 4)}
 
 

time: 47.9 us -> 47.1 us (0.983)
  the two profiles are of different devices: /device:TPU:56 before, /device:TPU:0 now
where the time goes in v5:
time: 47.1 us; the launch traced here: 46.3 us
  Pallas kernels  45.7 us (97%)
  between operations  0.64 us (1%)
    pallas_call x1, Pallas kernels, body(): pl.pallas_call(kernel, out_shape=(pltpu.VMEM((8, 512), f32), pltpu.VMEM((...  44.7 us
    pallas_call x1, Pallas kernels, body(): pl.pallas_call(store, out_shape=tuple((jax.ShapeDtypeStruct(field.shape,...  1 us

profile of v5, /device:TPU:0, one launch (start us, length us, event | category | flops | bytes accessed | tf_op | source)
XLA Modules:
  0.0 46.3 jit_solution(10878788263661663965)
XLA Ops:
  0.6 44.7 %shard_map.49 = (f32[8,512]{1,0:T(8,128)S(1)}, f32[8,512]{1,0:T(8,128)S(1)}, bf16[128,8,512]{2,1,0:T(8,128)(2,1)S(1)}) custom-call(f32[2,4,2,2,4,4,8,128]{7,6,5,4,3,2,1,0:T(8,128)} %bitcast.6, f32[2,4,2,2,4,4,8,128]{7,6,5,4,3,2,1,0:T(8,128)} %bitcast.7), custom_call_target="tpu_custom_call" | custom-call | tf_op jit(solution)/shard_map/pallas_call | solution.py:343
  45.3 1.0 %shard_map.50 = (f32[8,512]{1,0:T(8,128)}, f32[8,512]{1,0:T(8,128)}, bf16[128,8,512]{2,1,0:T(8,128)(2,1)}) custom-call(f32[8,512]{1,0:T(8,128)S(1)} %get-tuple-element.6.slope_ref, f32[8,512]{1,0:T(8,128)S(1)} %get-tuple-element.7.level_ref, bf16[128,8,512]{2,1,0:T(8,128)(2,1)S(1)} %get-tuple-element.8.anomaly_ref), custom_call_target="tpu_custom_call" | custom-call | tf_op jit(solution)/shard_map/pallas_call | solution.py:371

commit v6 on v5

--- a/solution.py
+++ b/solution.py
@@ -115,9 +115,10 @@
     for n, axis, q, c in everyone:
         greet(q < here[axis], seen_sem.at[8 * n + 2 * here[axis] + core], device_of(moved(**{axis: q}), c))
     greet(core == 0, seen_sem.at[24], device_of(here, 1))
-    heard = set()
+    heard, sender = set(), [0]
 
     def hear(condition, key, index):
+        key = (sender[0], key)
         if key not in heard:
             heard.add(key)
 
@@ -173,7 +174,9 @@
             for shift, which in ((0, 0), (0, 1), (1, 0), (1, 1), (2, 0), (2, 1), (None, 0), (None, 1)):
                 for c in range(2):
                     queues[ORDERS[piece][c][0]].append(functools.partial(near_copy, piece, c, shift, which))
-        return merge([queue for queue in queues.values() if queue])
+        lists = list(queues.values())
+        turned = 2 * sender[0]
+        return merge([queue for queue in lists[turned:] + lists[:turned] if queue])
 
     def merge(lists):
         ranked = [((i + 0.5) / len(items), n, item) for n, items in enumerate(lists) for i, item in enumerate(items)]
@@ -313,8 +316,15 @@
         else:
             pairs = [(name[i], int(name[i + 1])) for i in range(0, len(name), 2)]
             near = [piece for kind, piece in pairs if kind == "S"]
-            lists = [near_copies(near)] if near else []
-            for copy in merge(lists + [series_copies(kind, piece) for kind, piece in pairs if kind != "S"]):
+            if near:
+                for sender[0] in range(2):
+
+                    @pl.when(core == sender[0])
+                    def _():
+                        for copy in near_copies(near):
+                            copy()
+
+            for copy in merge([series_copies(kind, piece) for kind, piece in pairs if kind != "S"]):
                 copy()
 
     await_bytes(y_near.at[:, pl.ds(0, 7)], send_sem.at[0])

time: 47.1 us -> 47 us (level)
  no operation moved by 1% of the time
where the time goes in v6:
time: 47 us; the launch traced here: 46.2 us
  Pallas kernels  45.6 us (97%)
  between operations  0.64 us (1%)
    pallas_call x1, Pallas kernels, body(): pl.pallas_call(kernel, out_shape=(pltpu.VMEM((8, 512), f32), pltpu.VMEM((...  44.6 us
    pallas_call x1, Pallas kernels, body(): pl.pallas_call(store, out_shape=tuple((jax.ShapeDtypeStruct(field.shape,...  1 us

profile of v6, /device:TPU:0, one launch (start us, length us, event | category | flops | bytes accessed | tf_op | source)
XLA Modules:
  0.0 46.2 jit_solution(14688352157889774402)
XLA Ops:
  0.6 44.6 %shard_map.49 = (f32[8,512]{1,0:T(8,128)S(1)}, f32[8,512]{1,0:T(8,128)S(1)}, bf16[128,8,512]{2,1,0:T(8,128)(2,1)S(1)}) custom-call(f32[2,4,2,2,4,4,8,128]{7,6,5,4,3,2,1,0:T(8,128)} %bitcast.6, f32[2,4,2,2,4,4,8,128]{7,6,5,4,3,2,1,0:T(8,128)} %bitcast.7), custom_call_target="tpu_custom_call" | custom-call | tf_op jit(solution)/shard_map/pallas_call | solution.py:353
  45.2 1.0 %shard_map.50 = (f32[8,512]{1,0:T(8,128)}, f32[8,512]{1,0:T(8,128)}, bf16[128,8,512]{2,1,0:T(8,128)(2,1)}) custom-call(f32[8,512]{1,0:T(8,128)S(1)} %get-tuple-element.6.slope_ref, f32[8,512]{1,0:T(8,128)S(1)} %get-tuple-element.7.level_ref, bf16[128,8,512]{2,1,0:T(8,128)(2,1)S(1)} %get-tuple-element.8.anomaly_ref), custom_call_target="tpu_custom_call" | custom-call | tf_op jit(solution)/shard_map/pallas_call | solution.py:381

commit v7 on v6

--- a/solution.py
+++ b/solution.py
@@ -9,6 +9,7 @@
 
 MESH = pl.DeviceIdType.MESH
 PIECES = 4
+PARTS = 4
 LANES = 128
 ORDERS = (("xzy", "yzx"), ("zyx", "xzy"), ("yxz", "zyx"), ("xzy", "yxz"))
 OFFSETS = ((0, 0), (0, 1), (1, 0), (0, None), (None, 0), (0, 2), (1, 1), (2, 0), (None, 1), (1, None), (1, 2), (2, 1), (None, 2), (2, None), (2, 2))
@@ -335,7 +336,11 @@
 
 
 def store(slope_ref, level_ref, anomaly_ref, slope_out, level_out, anomaly_out, sem):
-    pairs = ((anomaly_ref, anomaly_out), (slope_ref, slope_out), (level_ref, level_out))
+    steps = anomaly_ref.shape[0] // PARTS
+    pairs = [(slope_ref, slope_out), (level_ref, level_out)]
+    for part in range(PARTS):
+        rows = pl.ds(part * steps, steps)
+        pairs.append((anomaly_ref.at[rows], anomaly_out.at[rows]))
     copies = [pltpu.make_async_copy(source, target, sem.at[i]) for i, (source, target) in enumerate(pairs)]
     for copy in copies:
         copy.start()
@@ -383,7 +388,7 @@
         out_shape=tuple(jax.ShapeDtypeStruct(field.shape, field.dtype) for field in fitted),
         in_specs=[pl.BlockSpec(memory_space=pltpu.VMEM)] * 3,
         out_specs=(pl.BlockSpec(memory_space=pl.ANY),) * 3,
-        scratch_shapes=[pltpu.SemaphoreType.DMA((3,))],
+        scratch_shapes=[pltpu.SemaphoreType.DMA((2 + PARTS,))],
     )(*(pltpu.with_memory_space_constraint(field, pltpu.VMEM) for field in fitted))
 
 

time: 47 us -> 47.1 us (level)
  no operation moved by 1% of the time
where the time goes in v7:
time: 47.1 us; the launch traced here: 46.2 us
  Pallas kernels  45.6 us (97%)
  between operations  0.64 us (1%)
    pallas_call x1, Pallas kernels, body(): pl.pallas_call(kernel, out_shape=(pltpu.VMEM((8, 512), f32), pltpu.VMEM((...  44.6 us
    pallas_call x1, Pallas kernels, body(): pl.pallas_call(store, out_shape=tuple((jax.ShapeDtypeStruct(field.shape,...  1.03 us

profile of v7, /device:TPU:0, one launch (start us, length us, event | category | flops | bytes accessed | tf_op | source)
XLA Modules:
  0.0 46.2 jit_solution(5499336794219369706)
XLA Ops:
  0.6 44.6 %shard_map.49 = (f32[8,512]{1,0:T(8,128)S(1)}, f32[8,512]{1,0:T(8,128)S(1)}, bf16[128,8,512]{2,1,0:T(8,128)(2,1)S(1)}) custom-call(f32[2,4,2,2,4,4,8,128]{7,6,5,4,3,2,1,0:T(8,128)} %bitcast.6, f32[2,4,2,2,4,4,8,128]{7,6,5,4,3,2,1,0:T(8,128)} %bitcast.7), custom_call_target="tpu_custom_call" | custom-call | tf_op jit(solution)/shard_map/pallas_call | solution.py:358
  45.2 1.0 %shard_map.50 = (f32[8,512]{1,0:T(8,128)}, f32[8,512]{1,0:T(8,128)}, bf16[128,8,512]{2,1,0:T(8,128)(2,1)}) custom-call(f32[8,512]{1,0:T(8,128)S(1)} %get-tuple-element.6.slope_ref, f32[8,512]{1,0:T(8,128)S(1)} %get-tuple-element.7.level_ref, bf16[128,8,512]{2,1,0:T(8,128)(2,1)S(1)} %get-tuple-element.8.anomaly_ref), custom_call_target="tpu_custom_call" | custom-call | tf_op jit(solution)/shard_map/pallas_call | solution.py:386
